TPU v7x, 32 devices: a whole 2x2x4 slice. The times are simulated.
32 devices in a mesh: img: 8 (over y, x, core), atom: 4 (over z).
Axes of the slice: x: 2, y: 2, z: 4, core: 2. Of those that a mesh axis runs over, the one named last changes fastest.
Arguments:
- positions: float32 [3, 256, 4096], P(None, 'img', 'atom'), may hold values from -6 to 6
- strength: float32 [4096], replicated, may hold values from 0.5 to 2
- tile_pairs: int32 [32, 8], replicated, may hold values from 0 to 31
- source_segment: int32 [256], P('img'), may hold values from 1 to 255, as said below
Outputs:
- string: float32 [3, 256, 4096], P(None, 'img', 'atom')
Inputs may be any that keep to these rules, and one draw needn't show every extreme that they name: source_segment[j] is j or j + 1, never 0 and never above 255.
All inputs are finite; a program needn't handle non-finite values.
Results may differ from a plain program's by a relative error of at most 0.0003.
Values sent between devices are 32-bit elements; how exact they have to be, the bound alone decides.
No kernel may reach another device: no remote copies, remote signals or barrier semaphores. Data moves between devices by JAX's collectives and lax.ppermute only.
A program may use at most 64 MiB of HBM per device.

v0:
```python
import jax
import jax.numpy as jnp
from jax import lax
from jax.sharding import PartitionSpec as P

TB = 128
STEP_SIZE = 0.02


def padded(cells, sides, width):
    for axis, dim in sides:
        count = lax.axis_size(axis)
        ends = count - 1
        head = lax.slice_in_dim(cells, 0, width, axis=dim)
        tail = lax.slice_in_dim(cells, cells.shape[dim] - width, cells.shape[dim], axis=dim)
        cells = jnp.concatenate(
            [
                lax.ppermute(tail, axis, [(i, (i + 1) % count) for i in range(ends)]),
                cells,
                lax.ppermute(head, axis, [((i + 1) % count, i) for i in range(ends)]),
            ],
            axis=dim,
        )
    return cells


def pair_force(block_pos, block_strength, whole_pos, strength, partners):
    force_sum = jnp.zeros(block_pos.shape, jnp.float32)
    for neighbor_slot in range(partners.shape[0]):
        first_atom = partners[neighbor_slot] * TB
        partner_pos = lax.dynamic_slice_in_dim(whole_pos, first_atom, TB, 2)
        partner_strength = lax.dynamic_slice_in_dim(strength, first_atom, TB, 0)
        differ = block_pos[:, :, :, None] - partner_pos[:, :, None, :]
        radius = jnp.sum(differ * differ, axis=0)
        coupling = (
            block_strength[None, :, None] * partner_strength[None, None, :] * jnp.exp(-0.5 * radius)
        )
        force_sum = force_sum + jnp.sum(differ * coupling[None], axis=3)
    return force_sum


def block_forces(blocks, indices, strength, tile_pairs, whole_pos):

    def one_block(inputs):
        block_pos, index = inputs
        partners = tile_pairs[index]
        block_strength = lax.dynamic_slice_in_dim(strength, index * TB, TB, 0)
        return pair_force(block_pos, block_strength, whole_pos, strength, partners)

    result = lax.map(one_block, (blocks, indices))
    block_count, _, image_count, _ = result.shape
    return result.transpose(1, 2, 0, 3).reshape(3, image_count, block_count * TB)


def shards(positions, strength, tile_pairs, source_segment):
    count = positions.shape[1]
    local_atoms = positions.shape[2]
    whole_pos = lax.all_gather(positions, "atom", axis=2, tiled=True)
    per_device = local_atoms // TB
    blocks = positions.reshape(3, count, per_device, TB).transpose(2, 0, 1, 3)
    indices = lax.axis_index("atom") * per_device + jnp.arange(per_device, dtype=jnp.int32)
    forces = block_forces(blocks, indices, strength, tile_pairs, whole_pos)
    moved = positions + STEP_SIZE * forces
    first_image = lax.axis_index("img") * count
    images_total = count * lax.axis_size("img")
    extended = padded(moved, (("img", 1),), 1)
    segments = extended[:, 1:] - extended[:, :-1]
    partial_value = jnp.sum(segments * segments, axis=(0, 2))
    squares = lax.psum(partial_value, "atom")
    global_ids = first_image + jnp.arange(count + 1, dtype=jnp.int32)
    valid = (global_ids >= 1) & (global_ids <= images_total - 1)
    lengths = jnp.where(valid, jnp.sqrt(1.0 + squares), jnp.zeros_like(squares))
    running = jnp.cumsum(lengths[:count])
    device_total = running[-1]
    totals = lax.all_gather(device_total[None], "img", axis=0, tiled=True)
    ranks = jnp.arange(totals.shape[0], dtype=jnp.int32)
    offset = jnp.sum(jnp.where(ranks < lax.axis_index("img"), totals, jnp.zeros_like(totals)))
    total_arc = jnp.sum(totals)
    arc_ext = jnp.concatenate(
        [offset[None], offset + running, (offset + device_total + lengths[count])[None]]
    )
    length_ext = jnp.concatenate([jnp.zeros((1,), jnp.float32), lengths])
    upper = source_segment - first_image + 1
    lower = upper - 1
    columns = jnp.arange(count + 2, dtype=jnp.int32)
    hit_low = (columns[None, :] == lower[:, None]).astype(jnp.float32)
    hit_high = (columns[None, :] == upper[:, None]).astype(jnp.float32)
    arc_low = jnp.sum(hit_low * arc_ext[None, :], axis=1)
    seg_length = jnp.sum(hit_high * length_ext[None, :], axis=1)
    target = (first_image + jnp.arange(count, dtype=jnp.int32)).astype(jnp.float32) * (
        total_arc / (images_total - 1)
    )
    weight = (target - arc_low) / seg_length
    mixing = (1.0 - weight)[:, None] * hit_low + weight[:, None] * hit_high
    string = jnp.einsum("je,cea->cja", mixing, extended, precision=lax.Precision.HIGHEST)
    return string


def solution(mesh):
    placed = (P(None, "img", "atom"), P(), P(), P("img"))
    return jax.shard_map(
        shards, mesh=mesh, in_specs=placed, out_specs=P(None, "img", "atom"), check_vma=False
    )
```

profile of v0, /device:TPU:4, one launch (start us, length us, event | category | flops | bytes accessed | tf_op | source)
XLA Modules:
  0.0 445.7 jit_solution(13500189040580754193)
XLA Ops:
  8.4 38.8 %all-gather.3.cloned.1.call-done = f32[3,32,4096]{2,1,0:T(8,128)} async-done(((f32[3,32,1024]{2,1,0:T(8,128)}), f32[3,32,4096]{2,1,0:T(8,128)}) %all-gather.3.cloned.1.call-update) | async-done | bytes 1572880 | tf_op jit(solution)/shard_map/all_gather | solution.py:58
  47.2 351.6 %while.10 = (s32[]{:T(128)}, f32[8,3,32,128]{3,2,1,0:T(8,128)}, f32[8,3,32,128]{3,0,2,1:T(8,128)S(1)}, s32[8]{0:T(128)S(1)}, s32[32,8]{0,1:T(8,128)}, /*index=5*...) while((s32[]{:T(128)}, f32[8,3,32,128]{3,2,1,0:T(8,128)}, ...), condition=%wide.region_17.18_spmd, body=%wide.region_0.17_spmd.sunk | while | flops 79810600 | bytes 70826768 | solution.py:50
  56.9 3.7 fusion.45
  64.4 10.2 %fusion.47 = (f32[3,32,128]{2,1,0:T(8,128)S(1)}, f32[32,128,128]{2,1,0:T(8,128)S(1)}, f32[32,128,128]{2,1,0:T(8,128)S(1)}, f32[32,128,128]{2,1,0:T(8,128)S(1)}, ...) fusion(f32[32,128,128]{2,1,0:T(8,128)S(1)} %get-tuple-element.2, ...), kind=kLoop, calls=%fused_computation.19.clone.1 | loop fusion | flops 34578432 | bytes 17317888 | tf_op jit(solution)/shard_map/while/body/eval_jaxpr/reduce_sum | solution.py:38
  76.3 14.1 %fusion.48 = (f32[3,32,128]{2,1,0:T(8,128)S(1)}, f32[3,32,128]{2,1,0:T(8,128)S(1)}, f32[3,32,128]{2,1,0:T(8,128)S(1)}, f32[3,32,128]{2,1,0:T(8,128)S(1)}, f32[3,...) fusion(f32[32,128,128]{2,1,0:T(8,128)S(1)} %exponential_multiply_fusion.16, ...), kind=kLoop, calls=%fused_computation.21.clone.1 | loop fusion | flops 28237824 | bytes 13221888 | tf_op jit(solution)/shard_map/while/body/eval_jaxpr/reduce_sum | solution.py:38
  100.9 3.7 fusion.45
  108.4 10.2 %fusion.47 = (f32[3,32,128]{2,1,0:T(8,128)S(1)}, f32[32,128,128]{2,1,0:T(8,128)S(1)}, f32[32,128,128]{2,1,0:T(8,128)S(1)}, f32[32,128,128]{2,1,0:T(8,128)S(1)}, ...) fusion(f32[32,128,128]{2,1,0:T(8,128)S(1)} %get-tuple-element.2, ...), kind=kLoop, calls=%fused_computation.19.clone.1 | loop fusion | flops 34578432 | bytes 17317888 | tf_op jit(solution)/shard_map/while/body/eval_jaxpr/reduce_sum | solution.py:38
  120.3 14.1 %fusion.48 = (f32[3,32,128]{2,1,0:T(8,128)S(1)}, f32[3,32,128]{2,1,0:T(8,128)S(1)}, f32[3,32,128]{2,1,0:T(8,128)S(1)}, f32[3,32,128]{2,1,0:T(8,128)S(1)}, f32[3,...) fusion(f32[32,128,128]{2,1,0:T(8,128)S(1)} %exponential_multiply_fusion.16, ...), kind=kLoop, calls=%fused_computation.21.clone.1 | loop fusion | flops 28237824 | bytes 13221888 | tf_op jit(solution)/shard_map/while/body/eval_jaxpr/reduce_sum | solution.py:38
  152.3 10.2 %fusion.47 = (f32[3,32,128]{2,1,0:T(8,128)S(1)}, f32[32,128,128]{2,1,0:T(8,128)S(1)}, f32[32,128,128]{2,1,0:T(8,128)S(1)}, f32[32,128,128]{2,1,0:T(8,128)S(1)}, ...) fusion(f32[32,128,128]{2,1,0:T(8,128)S(1)} %get-tuple-element.2, ...), kind=kLoop, calls=%fused_computation.19.clone.1 | loop fusion | flops 34578432 | bytes 17317888 | tf_op jit(solution)/shard_map/while/body/eval_jaxpr/reduce_sum | solution.py:38
  164.2 14.1 %fusion.48 = (f32[3,32,128]{2,1,0:T(8,128)S(1)}, f32[3,32,128]{2,1,0:T(8,128)S(1)}, f32[3,32,128]{2,1,0:T(8,128)S(1)}, f32[3,32,128]{2,1,0:T(8,128)S(1)}, f32[3,...) fusion(f32[32,128,128]{2,1,0:T(8,128)S(1)} %exponential_multiply_fusion.16, ...), kind=kLoop, calls=%fused_computation.21.clone.1 | loop fusion | flops 28237824 | bytes 13221888 | tf_op jit(solution)/shard_map/while/body/eval_jaxpr/reduce_sum | solution.py:38
  188.7 3.7 fusion.45
  196.2 10.2 %fusion.47 = (f32[3,32,128]{2,1,0:T(8,128)S(1)}, f32[32,128,128]{2,1,0:T(8,128)S(1)}, f32[32,128,128]{2,1,0:T(8,128)S(1)}, f32[32,128,128]{2,1,0:T(8,128)S(1)}, ...) fusion(f32[32,128,128]{2,1,0:T(8,128)S(1)} %get-tuple-element.2, ...), kind=kLoop, calls=%fused_computation.19.clone.1 | loop fusion | flops 34578432 | bytes 17317888 | tf_op jit(solution)/shard_map/while/body/eval_jaxpr/reduce_sum | solution.py:38
  208.1 14.1 %fusion.48 = (f32[3,32,128]{2,1,0:T(8,128)S(1)}, f32[3,32,128]{2,1,0:T(8,128)S(1)}, f32[3,32,128]{2,1,0:T(8,128)S(1)}, f32[3,32,128]{2,1,0:T(8,128)S(1)}, f32[3,...) fusion(f32[32,128,128]{2,1,0:T(8,128)S(1)} %exponential_multiply_fusion.16, ...), kind=kLoop, calls=%fused_computation.21.clone.1 | loop fusion | flops 28237824 | bytes 13221888 | tf_op jit(solution)/shard_map/while/body/eval_jaxpr/reduce_sum | solution.py:38
  240.1 10.2 %fusion.47 = (f32[3,32,128]{2,1,0:T(8,128)S(1)}, f32[32,128,128]{2,1,0:T(8,128)S(1)}, f32[32,128,128]{2,1,0:T(8,128)S(1)}, f32[32,128,128]{2,1,0:T(8,128)S(1)}, ...) fusion(f32[32,128,128]{2,1,0:T(8,128)S(1)} %get-tuple-element.2, ...), kind=kLoop, calls=%fused_computation.19.clone.1 | loop fusion | flops 34578432 | bytes 17317888 | tf_op jit(solution)/shard_map/while/body/eval_jaxpr/reduce_sum | solution.py:38
  252.0 14.1 %fusion.48 = (f32[3,32,128]{2,1,0:T(8,128)S(1)}, f32[3,32,128]{2,1,0:T(8,128)S(1)}, f32[3,32,128]{2,1,0:T(8,128)S(1)}, f32[3,32,128]{2,1,0:T(8,128)S(1)}, f32[3,...) fusion(f32[32,128,128]{2,1,0:T(8,128)S(1)} %exponential_multiply_fusion.16, ...), kind=kLoop, calls=%fused_computation.21.clone.1 | loop fusion | flops 28237824 | bytes 13221888 | tf_op jit(solution)/shard_map/while/body/eval_jaxpr/reduce_sum | solution.py:38
  284.0 10.2 %fusion.47 = (f32[3,32,128]{2,1,0:T(8,128)S(1)}, f32[32,128,128]{2,1,0:T(8,128)S(1)}, f32[32,128,128]{2,1,0:T(8,128)S(1)}, f32[32,128,128]{2,1,0:T(8,128)S(1)}, ...) fusion(f32[32,128,128]{2,1,0:T(8,128)S(1)} %get-tuple-element.2, ...), kind=kLoop, calls=%fused_computation.19.clone.1 | loop fusion | flops 34578432 | bytes 17317888 | tf_op jit(solution)/shard_map/while/body/eval_jaxpr/reduce_sum | solution.py:38
  296.0 14.1 %fusion.48 = (f32[3,32,128]{2,1,0:T(8,128)S(1)}, f32[3,32,128]{2,1,0:T(8,128)S(1)}, f32[3,32,128]{2,1,0:T(8,128)S(1)}, f32[3,32,128]{2,1,0:T(8,128)S(1)}, f32[3,...) fusion(f32[32,128,128]{2,1,0:T(8,128)S(1)} %exponential_multiply_fusion.16, ...), kind=kLoop, calls=%fused_computation.21.clone.1 | loop fusion | flops 28237824 | bytes 13221888 | tf_op jit(solution)/shard_map/while/body/eval_jaxpr/reduce_sum | solution.py:38
  328.0 10.2 %fusion.47 = (f32[3,32,128]{2,1,0:T(8,128)S(1)}, f32[32,128,128]{2,1,0:T(8,128)S(1)}, f32[32,128,128]{2,1,0:T(8,128)S(1)}, f32[32,128,128]{2,1,0:T(8,128)S(1)}, ...) fusion(f32[32,128,128]{2,1,0:T(8,128)S(1)} %get-tuple-element.2, ...), kind=kLoop, calls=%fused_computation.19.clone.1 | loop fusion | flops 34578432 | bytes 17317888 | tf_op jit(solution)/shard_map/while/body/eval_jaxpr/reduce_sum | solution.py:38
  339.9 14.1 %fusion.48 = (f32[3,32,128]{2,1,0:T(8,128)S(1)}, f32[3,32,128]{2,1,0:T(8,128)S(1)}, f32[3,32,128]{2,1,0:T(8,128)S(1)}, f32[3,32,128]{2,1,0:T(8,128)S(1)}, f32[3,...) fusion(f32[32,128,128]{2,1,0:T(8,128)S(1)} %exponential_multiply_fusion.16, ...), kind=kLoop, calls=%fused_computation.21.clone.1 | loop fusion | flops 28237824 | bytes 13221888 | tf_op jit(solution)/shard_map/while/body/eval_jaxpr/reduce_sum | solution.py:38
  372.0 10.2 %fusion.47 = (f32[3,32,128]{2,1,0:T(8,128)S(1)}, f32[32,128,128]{2,1,0:T(8,128)S(1)}, f32[32,128,128]{2,1,0:T(8,128)S(1)}, f32[32,128,128]{2,1,0:T(8,128)S(1)}, ...) fusion(f32[32,128,128]{2,1,0:T(8,128)S(1)} %get-tuple-element.2, ...), kind=kLoop, calls=%fused_computation.19.clone.1 | loop fusion | flops 34578432 | bytes 17317888 | tf_op jit(solution)/shard_map/while/body/eval_jaxpr/reduce_sum | solution.py:38
  383.9 14.1 %fusion.48 = (f32[3,32,128]{2,1,0:T(8,128)S(1)}, f32[3,32,128]{2,1,0:T(8,128)S(1)}, f32[3,32,128]{2,1,0:T(8,128)S(1)}, f32[3,32,128]{2,1,0:T(8,128)S(1)}, f32[3,...) fusion(f32[32,128,128]{2,1,0:T(8,128)S(1)} %exponential_multiply_fusion.16, ...), kind=kLoop, calls=%fused_computation.21.clone.1 | loop fusion | flops 28237824 | bytes 13221888 | tf_op jit(solution)/shard_map/while/body/eval_jaxpr/reduce_sum | solution.py:38
  401.7 4.5 %collective-permute-start.1 = (f32[3,1,1024]{2,1,0:T(1,128)S(1)}, f32[3,1,1024]{2,1,0:T(1,128)S(1)}, u32[]{:S(2)}, u32[]{:S(2)}) collective-permute-start(f32[3,1,1024]{2,1,0:T(1,128)S(1)} %get-tuple-element.129), channel_id=1, source_target_pairs={{4,0},{8,4},{12,8},{16,12},{20,16},{24,20},{28,24},{5,1},{9,5},{13... | collective-permute-start | bytes 36872 | tf_op jit(solution)/shard_map/ppermute | solution.py:20
  407.9 9.6 %psum.7 = f32[33]{0:T(128)S(1)} all-reduce(f32[33]{0:T(128)S(1)} %fusion.22), channel_id=1, replica_groups=mesh['img'=8,'atom'=4] {'atom'}, use_global_device_ids=true, to_apply=%region_19.20 | all-reduce | flops 33 | bytes 264 | tf_op jit(solution)/shard_map/psum | solution.py:69
  420.1 12.4 %all-reduce = f32[8]{0:T(128)S(1)} all-reduce(f32[8]{0:T(128)S(1)} %bitcast_dynamic-update-slice_fusion.1), channel_id=2, replica_groups=mesh['img'=8,'atom'=4] {'img'}, use_global_device_ids=true, to_apply=%add | all-reduce | flops 8 | bytes 64 | tf_op jit(solution)/shard_map/all_gather | solution.py:75
  (160 shorter events, 99.9 us)
Async XLA Ops:
  6.5 40.6 %all-gather.3.cloned.1.call-start = ((), (), s32[]{:S(2)}) async-start(), calls=%async_computation | async-start | bytes 1966080 | tf_op jit(solution)/shard_map/all_gather | solution.py:58
  47.2 351.6 %copy-start = (f32[3,32,1024]{2,1,0:T(8,128)S(1)}, f32[3,32,1024]{2,1,0:T(8,128)}, u32[]{:S(2)}) copy-start(f32[3,32,1024]{2,1,0:T(8,128)} %param.6) | copy-start | bytes 1179652
  47.2 359.1 %copy-start.1 = (s32[32]{0:T(128)S(1)}, s32[32]{0:T(128)}, u32[]{:S(2)}) copy-start(s32[32]{0:T(128)} %param.9) | copy-start | bytes 388
  47.2 359.1 %copy-start.2 = (u32[32]{0:T(128)S(1)}, u32[32]{0:T(128)}, u32[]{:S(2)}) copy-start(u32[32]{0:T(128)} %constant.75) | copy-start | bytes 388
  399.8 7.1 %collective-permute-start = (f32[3,1,1024]{2,1,0:T(1,128)S(1)}, f32[3,1,1024]{2,1,0:T(1,128)S(1)}, u32[]{:S(2)}, u32[]{:S(2)}) collective-permute-start(f32[3,1,1024]{2,1,0:T(1,128)S(1)} %get-tuple-element.128), channel_id=1, source_target_pairs={{0,4},{4,8},{8,12},{12,16},{16,20},{20,24},{24,28},{1,5},{5,9},{9,... | collective-permute-start | bytes 36872 | tf_op jit(solution)/shard_map/ppermute | solution.py:18
  401.7 5.9 %collective-permute-start.1 = (f32[3,1,1024]{2,1,0:T(1,128)S(1)}, f32[3,1,1024]{2,1,0:T(1,128)S(1)}, u32[]{:S(2)}, u32[]{:S(2)}) collective-permute-start(f32[3,1,1024]{2,1,0:T(1,128)S(1)} %get-tuple-element.129), channel_id=1, source_target_pairs={{4,0},{8,4},{12,8},{16,12},{20,16},{24,20},{28,24},{5,1},{9,5},{13... | collective-permute-start | bytes 36872 | tf_op jit(solution)/shard_map/ppermute | solution.py:20
Sparse Core Ops, SparseCore 0:
  8.9 38.2 all-gather.2
where the time goes:
time: 448 us; the launch traced here: 446 us
  other arithmetic  264 us (59%)
  loops' own time  58.9 us (13%)
  waiting for transfers between devices  40.2 us (9%)
  local copies, waits for them, and re-layouts  36.3 us (8%)
  blocking collectives  22 us (5%)
  between operations  16.1 us (4%)
  starting transfers between devices  6.46 us (1%)
    reduce_sum x16, other arithmetic, pair_force(): force_sum = force_sum + jnp.sum(differ * coupling[None], axis=3)  194 us
    another operation x1, loops' own time, block_forces(): result = lax.map(one_block, (blocks, indices))  58.9 us
    all_gather x1, waiting for transfers between devices, shards(): whole_pos = lax.all_gather(positions, 'atom', axis=2, tiled=True)  38.8 us
    mul x64, other arithmetic, pair_force(): block_strength[None, :, None] * partner_strength[None, None, :]  31.5 us
    reduce_sum x8, other arithmetic, pair_force(): radius = jnp.sum(differ * differ, axis=0)  29.4 us
    all_gather x1, blocking collectives, shards(): totals = lax.all_gather(device_total[None], 'img', axis=0, tiled=True)  12.4 us
    psum x1, blocking collectives, shards(): squares = lax.psum(partial_value, 'atom')  9.62 us
  transfers between devices with their start and end apart: 3, of which 2 were waited for; matrix products, arithmetic and copies ran while one was open for 0% of the time, Pallas kernels for 0%

commit v1 on v0

--- a/solution.py
+++ b/solution.py
@@ -5,6 +5,22 @@
 
 TB = 128
 STEP_SIZE = 0.02
+
+
+def treat_cube(inp, axis_no):
+    many = lax.psum(1, "atom")
+    state_next = range(many)
+    side_arr = map(lambda d: (d, (d + 1) % many), state_next)
+    line_up = list(side_arr)
+
+    def fill_object(n_now):
+        if len(n_now) == many:
+            return n_now
+        return fill_object([lax.ppermute(n_now[0], "atom", line_up), *n_now])
+
+    mixed_arr = fill_object([inp])
+    p_next = jnp.concatenate(mixed_arr, axis=axis_no)
+    return jnp.roll(p_next, (lax.axis_index("atom") + 1) * inp.shape[axis_no], axis=axis_no)
 
 
 def padded(cells, sides, width):
@@ -55,7 +71,7 @@
 def shards(positions, strength, tile_pairs, source_segment):
     count = positions.shape[1]
     local_atoms = positions.shape[2]
-    whole_pos = lax.all_gather(positions, "atom", axis=2, tiled=True)
+    whole_pos = treat_cube(positions, 2)
     per_device = local_atoms // TB
     blocks = positions.reshape(3, count, per_device, TB).transpose(2, 0, 1, 3)
     indices = lax.axis_index("atom") * per_device + jnp.arange(per_device, dtype=jnp.int32)

time: 448 us -> 417 us (0.931)
  between operations: 16.1 us -> 2.75 us
  local copies, waits for them, and re-layouts: 36.3 us -> 24.4 us
  waiting for transfers between devices: 40.2 us -> 34 us
    all_gather x1 -> x0, waiting for transfers between devices: 38.8 us -> none  [shards(): whole_pos = lax.all_gather(positions, 'atom', axis=2, tiled=True)]
    ppermute x0 -> x3, waiting for transfers between devices: none -> 33.3 us  [fill_object(): return fill_object([lax.ppermute(n_now[0], 'atom', line_up), *n_now])]
    dynamic_slice x8, local copies, waits for them, and re-layouts: 8.23 us -> 0.58 us  [pair_force(): partner_pos = lax.dynamic_slice_in_dim(whole_pos, first_atom, TB, 2)]
    dynamic_slice x8, local copies, waits for them, and re-layouts: 6.1 us -> 0.59 us  [one_block(): partners = tile_pairs[index]]
  transfers between devices with their start and end apart: 3 -> 5, of which waited for: 2 -> 4; matrix products, arithmetic and copies ran while one was open for 0% -> 0% of each run, Pallas kernels for 0% -> 0%
where the time goes in v1:
time: 417 us; the launch traced here: 415 us
  other arithmetic  264 us (63%)
  loops' own time  59.1 us (14%)
  waiting for transfers between devices  34 us (8%)
  local copies, waits for them, and re-layouts  24.4 us (6%)
  blocking collectives  21 us (5%)
  starting transfers between devices  8.04 us (2%)
    reduce_sum x16, other arithmetic, pair_force(): force_sum = force_sum + jnp.sum(differ * coupling[None], axis=3)  194 us
    another operation x1, loops' own time, block_forces(): result = lax.map(one_block, (blocks, indices))  59.1 us
    ppermute x3, waiting for transfers between devices, fill_object(): return fill_object([lax.ppermute(n_now[0], 'atom', line_up), *n_now])  33.3 us
    mul x64, other arithmetic, pair_force(): block_strength[None, :, None] * partner_strength[None, None, :]  31.5 us
    reduce_sum x8, other arithmetic, pair_force(): radius = jnp.sum(differ * differ, axis=0)  29.4 us
    all_gather x1, blocking collectives, shards(): totals = lax.all_gather(device_total[None], 'img', axis=0, tiled=True)  12.6 us
    psum x1, blocking collectives, shards(): squares = lax.psum(partial_value, 'atom')  8.44 us
  transfers between devices with their start and end apart: 5, of which 4 were waited for; matrix products, arithmetic and copies ran while one was open for 0% of the time, Pallas kernels for 0%

profile of v1, /device:TPU:4, one launch (start us, length us, event | category | flops | bytes accessed | tf_op | source)
XLA Modules:
  0.0 415.1 jit_solution(17208141507518555670)
XLA Ops:
  1.6 11.4 %collective-permute-done = f32[3,32,1024]{2,1,0:T(8,128)S(1)} collective-permute-done((f32[3,32,1024]{2,1,0:T(8,128)}, f32[3,32,1024]{2,1,0:T(8,128)S(1)}, u32[]{:S(2)}, u32[]{:S(2)}) %collective-permute-start) | collective-permute-done | bytes 393248 | tf_op jit(solution)/shard_map/ppermute | solution.py:19
  13.0 11.9 %collective-permute-done.1 = f32[3,32,1024]{2,1,0:T(8,128)S(1)} collective-permute-done((f32[3,32,1024]{2,1,0:T(8,128)S(1)}, f32[3,32,1024]{2,1,0:T(8,128)S(1)}, u32[]{:S(2)}, u32[]{:S(2)}) %collective-permute-start.1) | collective-permute-done | bytes 393248 | tf_op jit(solution)/shard_map/ppermute | solution.py:19
  26.1 9.9 %collective-permute-done.2 = f32[3,32,1024]{2,1,0:T(8,128)S(1)} collective-permute-done((f32[3,32,1024]{2,1,0:T(8,128)S(1)}, f32[3,32,1024]{2,1,0:T(8,128)S(1)}, u32[]{:S(2)}, u32[]{:S(2)}) %collective-permute-start.2) | collective-permute-done | bytes 393248 | tf_op jit(solution)/shard_map/ppermute | solution.py:19
  36.8 339.1 %while.10 = (s32[]{:T(128)}, f32[8,3,32,128]{3,2,1,0:T(8,128)}, f32[8,3,32,128]{3,0,2,1:T(8,128)S(1)}, s32[8]{0:T(128)S(1)}, s32[32,8]{0,1:T(8,128)S(1)}, /*inde...) while((s32[]{:T(128)}, f32[8,3,32,128]{3,2,1,0:T(8,128)}, ...), condition=%wide.region_17.18_spmd, body=%wide.region_0.17_spmd.sunk | while | flops 79810600 | bytes 83409736 | solution.py:66
  52.5 10.2 %fusion.47 = (f32[3,32,128]{2,1,0:T(8,128)S(1)}, f32[32,128,128]{2,1,0:T(8,128)S(1)}, f32[32,128,128]{2,1,0:T(8,128)S(1)}, f32[32,128,128]{2,1,0:T(8,128)S(1)}, ...) fusion(f32[32,128,128]{2,1,0:T(8,128)S(1)} %get-tuple-element.2, ...), kind=kLoop, calls=%fused_computation.19.clone.1 | loop fusion | flops 34578432 | bytes 17317888 | tf_op jit(solution)/shard_map/while/body/eval_jaxpr/reduce_sum | solution.py:54
  64.4 14.1 %fusion.48 = (f32[3,32,128]{2,1,0:T(8,128)S(1)}, f32[3,32,128]{2,1,0:T(8,128)S(1)}, f32[3,32,128]{2,1,0:T(8,128)S(1)}, f32[3,32,128]{2,1,0:T(8,128)S(1)}, f32[3,...) fusion(f32[32,128,128]{2,1,0:T(8,128)S(1)} %exponential_multiply_fusion.16, ...), kind=kLoop, calls=%fused_computation.21.clone.1 | loop fusion | flops 28237824 | bytes 13221888 | tf_op jit(solution)/shard_map/while/body/eval_jaxpr/reduce_sum | solution.py:54
  94.9 10.2 %fusion.47 = (f32[3,32,128]{2,1,0:T(8,128)S(1)}, f32[32,128,128]{2,1,0:T(8,128)S(1)}, f32[32,128,128]{2,1,0:T(8,128)S(1)}, f32[32,128,128]{2,1,0:T(8,128)S(1)}, ...) fusion(f32[32,128,128]{2,1,0:T(8,128)S(1)} %get-tuple-element.2, ...), kind=kLoop, calls=%fused_computation.19.clone.1 | loop fusion | flops 34578432 | bytes 17317888 | tf_op jit(solution)/shard_map/while/body/eval_jaxpr/reduce_sum | solution.py:54
  106.8 14.1 %fusion.48 = (f32[3,32,128]{2,1,0:T(8,128)S(1)}, f32[3,32,128]{2,1,0:T(8,128)S(1)}, f32[3,32,128]{2,1,0:T(8,128)S(1)}, f32[3,32,128]{2,1,0:T(8,128)S(1)}, f32[3,...) fusion(f32[32,128,128]{2,1,0:T(8,128)S(1)} %exponential_multiply_fusion.16, ...), kind=kLoop, calls=%fused_computation.21.clone.1 | loop fusion | flops 28237824 | bytes 13221888 | tf_op jit(solution)/shard_map/while/body/eval_jaxpr/reduce_sum | solution.py:54
  129.8 3.7 fusion.45
  137.3 10.2 %fusion.47 = (f32[3,32,128]{2,1,0:T(8,128)S(1)}, f32[32,128,128]{2,1,0:T(8,128)S(1)}, f32[32,128,128]{2,1,0:T(8,128)S(1)}, f32[32,128,128]{2,1,0:T(8,128)S(1)}, ...) fusion(f32[32,128,128]{2,1,0:T(8,128)S(1)} %get-tuple-element.2, ...), kind=kLoop, calls=%fused_computation.19.clone.1 | loop fusion | flops 34578432 | bytes 17317888 | tf_op jit(solution)/shard_map/while/body/eval_jaxpr/reduce_sum | solution.py:54
  149.2 14.1 %fusion.48 = (f32[3,32,128]{2,1,0:T(8,128)S(1)}, f32[3,32,128]{2,1,0:T(8,128)S(1)}, f32[3,32,128]{2,1,0:T(8,128)S(1)}, f32[3,32,128]{2,1,0:T(8,128)S(1)}, f32[3,...) fusion(f32[32,128,128]{2,1,0:T(8,128)S(1)} %exponential_multiply_fusion.16, ...), kind=kLoop, calls=%fused_computation.21.clone.1 | loop fusion | flops 28237824 | bytes 13221888 | tf_op jit(solution)/shard_map/while/body/eval_jaxpr/reduce_sum | solution.py:54
  179.6 10.2 %fusion.47 = (f32[3,32,128]{2,1,0:T(8,128)S(1)}, f32[32,128,128]{2,1,0:T(8,128)S(1)}, f32[32,128,128]{2,1,0:T(8,128)S(1)}, f32[32,128,128]{2,1,0:T(8,128)S(1)}, ...) fusion(f32[32,128,128]{2,1,0:T(8,128)S(1)} %get-tuple-element.2, ...), kind=kLoop, calls=%fused_computation.19.clone.1 | loop fusion | flops 34578432 | bytes 17317888 | tf_op jit(solution)/shard_map/while/body/eval_jaxpr/reduce_sum | solution.py:54
  191.6 14.1 %fusion.48 = (f32[3,32,128]{2,1,0:T(8,128)S(1)}, f32[3,32,128]{2,1,0:T(8,128)S(1)}, f32[3,32,128]{2,1,0:T(8,128)S(1)}, f32[3,32,128]{2,1,0:T(8,128)S(1)}, f32[3,...) fusion(f32[32,128,128]{2,1,0:T(8,128)S(1)} %exponential_multiply_fusion.16, ...), kind=kLoop, calls=%fused_computation.21.clone.1 | loop fusion | flops 28237824 | bytes 13221888 | tf_op jit(solution)/shard_map/while/body/eval_jaxpr/reduce_sum | solution.py:54
  222.0 10.2 %fusion.47 = (f32[3,32,128]{2,1,0:T(8,128)S(1)}, f32[32,128,128]{2,1,0:T(8,128)S(1)}, f32[32,128,128]{2,1,0:T(8,128)S(1)}, f32[32,128,128]{2,1,0:T(8,128)S(1)}, ...) fusion(f32[32,128,128]{2,1,0:T(8,128)S(1)} %get-tuple-element.2, ...), kind=kLoop, calls=%fused_computation.19.clone.1 | loop fusion | flops 34578432 | bytes 17317888 | tf_op jit(solution)/shard_map/while/body/eval_jaxpr/reduce_sum | solution.py:54
  233.9 14.1 %fusion.48 = (f32[3,32,128]{2,1,0:T(8,128)S(1)}, f32[3,32,128]{2,1,0:T(8,128)S(1)}, f32[3,32,128]{2,1,0:T(8,128)S(1)}, f32[3,32,128]{2,1,0:T(8,128)S(1)}, f32[3,...) fusion(f32[32,128,128]{2,1,0:T(8,128)S(1)} %exponential_multiply_fusion.16, ...), kind=kLoop, calls=%fused_computation.21.clone.1 | loop fusion | flops 28237824 | bytes 13221888 | tf_op jit(solution)/shard_map/while/body/eval_jaxpr/reduce_sum | solution.py:54
  264.4 10.2 %fusion.47 = (f32[3,32,128]{2,1,0:T(8,128)S(1)}, f32[32,128,128]{2,1,0:T(8,128)S(1)}, f32[32,128,128]{2,1,0:T(8,128)S(1)}, f32[32,128,128]{2,1,0:T(8,128)S(1)}, ...) fusion(f32[32,128,128]{2,1,0:T(8,128)S(1)} %get-tuple-element.2, ...), kind=kLoop, calls=%fused_computation.19.clone.1 | loop fusion | flops 34578432 | bytes 17317888 | tf_op jit(solution)/shard_map/while/body/eval_jaxpr/reduce_sum | solution.py:54
  276.4 14.1 %fusion.48 = (f32[3,32,128]{2,1,0:T(8,128)S(1)}, f32[3,32,128]{2,1,0:T(8,128)S(1)}, f32[3,32,128]{2,1,0:T(8,128)S(1)}, f32[3,32,128]{2,1,0:T(8,128)S(1)}, f32[3,...) fusion(f32[32,128,128]{2,1,0:T(8,128)S(1)} %exponential_multiply_fusion.16, ...), kind=kLoop, calls=%fused_computation.21.clone.1 | loop fusion | flops 28237824 | bytes 13221888 | tf_op jit(solution)/shard_map/while/body/eval_jaxpr/reduce_sum | solution.py:54
  306.9 10.2 %fusion.47 = (f32[3,32,128]{2,1,0:T(8,128)S(1)}, f32[32,128,128]{2,1,0:T(8,128)S(1)}, f32[32,128,128]{2,1,0:T(8,128)S(1)}, f32[32,128,128]{2,1,0:T(8,128)S(1)}, ...) fusion(f32[32,128,128]{2,1,0:T(8,128)S(1)} %get-tuple-element.2, ...), kind=kLoop, calls=%fused_computation.19.clone.1 | loop fusion | flops 34578432 | bytes 17317888 | tf_op jit(solution)/shard_map/while/body/eval_jaxpr/reduce_sum | solution.py:54
  318.8 14.1 %fusion.48 = (f32[3,32,128]{2,1,0:T(8,128)S(1)}, f32[3,32,128]{2,1,0:T(8,128)S(1)}, f32[3,32,128]{2,1,0:T(8,128)S(1)}, f32[3,32,128]{2,1,0:T(8,128)S(1)}, f32[3,...) fusion(f32[32,128,128]{2,1,0:T(8,128)S(1)} %exponential_multiply_fusion.16, ...), kind=kLoop, calls=%fused_computation.21.clone.1 | loop fusion | flops 28237824 | bytes 13221888 | tf_op jit(solution)/shard_map/while/body/eval_jaxpr/reduce_sum | solution.py:54
  349.2 10.2 %fusion.47 = (f32[3,32,128]{2,1,0:T(8,128)S(1)}, f32[32,128,128]{2,1,0:T(8,128)S(1)}, f32[32,128,128]{2,1,0:T(8,128)S(1)}, f32[32,128,128]{2,1,0:T(8,128)S(1)}, ...) fusion(f32[32,128,128]{2,1,0:T(8,128)S(1)} %get-tuple-element.2, ...), kind=kLoop, calls=%fused_computation.19.clone.1 | loop fusion | flops 34578432 | bytes 17317888 | tf_op jit(solution)/shard_map/while/body/eval_jaxpr/reduce_sum | solution.py:54
  361.2 14.1 %fusion.48 = (f32[3,32,128]{2,1,0:T(8,128)S(1)}, f32[3,32,128]{2,1,0:T(8,128)S(1)}, f32[3,32,128]{2,1,0:T(8,128)S(1)}, f32[3,32,128]{2,1,0:T(8,128)S(1)}, f32[3,...) fusion(f32[32,128,128]{2,1,0:T(8,128)S(1)} %exponential_multiply_fusion.16, ...), kind=kLoop, calls=%fused_computation.21.clone.1 | loop fusion | flops 28237824 | bytes 13221888 | tf_op jit(solution)/shard_map/while/body/eval_jaxpr/reduce_sum | solution.py:54
  379.0 4.5 %collective-permute-start.4 = (f32[3,1,1024]{2,1,0:T(1,128)S(1)}, f32[3,1,1024]{2,1,0:T(1,128)S(1)}, u32[]{:S(2)}, u32[]{:S(2)}) collective-permute-start(f32[3,1,1024]{2,1,0:T(1,128)S(1)} %get-tuple-element.129), channel_id=1, source_target_pairs={{4,0},{8,4},{12,8},{16,12},{20,16},{24,20},{28,24},{5,1},{9,5},{13... | collective-permute-start | bytes 36872 | tf_op jit(solution)/shard_map/ppermute | solution.py:36
  385.1 8.4 %psum.7 = f32[33]{0:T(128)S(1)} all-reduce(f32[33]{0:T(128)S(1)} %fusion.22), channel_id=1, replica_groups=mesh['img'=8,'atom'=4] {'atom'}, use_global_device_ids=true, to_apply=%region_19.20 | all-reduce | flops 33 | bytes 264 | tf_op jit(solution)/shard_map/psum | solution.py:85
  396.2 12.6 %all-reduce = f32[8]{0:T(128)S(1)} all-reduce(f32[8]{0:T(128)S(1)} %bitcast_dynamic-update-slice_fusion.1), channel_id=2, replica_groups=mesh['img'=8,'atom'=4] {'img'}, use_global_device_ids=true, to_apply=%add | all-reduce | flops 8 | bytes 64 | tf_op jit(solution)/shard_map/all_gather | solution.py:91
  (206 shorter events, 96.3 us)
Async XLA Ops:
  0.0 36.1 %copy-start.2 = (f32[3,32,1024]{2,1,0:T(8,128)S(1)}, f32[3,32,1024]{2,1,0:T(8,128)}, u32[]{:S(2)}) copy-start(f32[3,32,1024]{2,1,0:T(8,128)} %param.6) | copy-start | bytes 1179652
  0.0 13.0 %collective-permute-start = (f32[3,32,1024]{2,1,0:T(8,128)}, f32[3,32,1024]{2,1,0:T(8,128)S(1)}, u32[]{:S(2)}, u32[]{:S(2)}) collective-permute-start(f32[3,32,1024]{2,1,0:T(8,128)} %param.6), channel_id=1, source_target_pairs={{0,1},{1,2},{2,3},{3,0},{4,5},{5,6},{6,7},{7,4},{8,9},{9,10},{10,1... | collective-permute-start | bytes 1179656 | tf_op jit(solution)/shard_map/ppermute | solution.py:19
  13.0 11.9 %collective-permute-start.1 = (f32[3,32,1024]{2,1,0:T(8,128)S(1)}, f32[3,32,1024]{2,1,0:T(8,128)S(1)}, u32[]{:S(2)}, u32[]{:S(2)}) collective-permute-start(f32[3,32,1024]{2,1,0:T(8,128)S(1)} %collective-permute-done), channel_id=1, source_target_pairs={{0,1},{1,2},{2,3},{3,0},{4,5},{5,6},{6,7},{7,4},{8,9},{9,10},{10,1... | collective-permute-start | bytes 1179656 | tf_op jit(solution)/shard_map/ppermute | solution.py:19
  24.9 11.1 %collective-permute-start.2 = (f32[3,32,1024]{2,1,0:T(8,128)S(1)}, f32[3,32,1024]{2,1,0:T(8,128)S(1)}, u32[]{:S(2)}, u32[]{:S(2)}) collective-permute-start(f32[3,32,1024]{2,1,0:T(8,128)S(1)} %collective-permute-done.1), channel_id=1, source_target_pairs={{0,1},{1,2},{2,3},{3,0},{4,5},{5,6},{6,7},{7,4},{8,9},{9,10},{10,1... | collective-permute-start | bytes 1179656 | tf_op jit(solution)/shard_map/ppermute | solution.py:19
  36.8 346.7 %copy-start.4 = (s32[32]{0:T(128)S(1)}, s32[32]{0:T(128)}, u32[]{:S(2)}) copy-start(s32[32]{0:T(128)} %param.9) | copy-start | bytes 388
  36.8 346.7 %copy-start.5 = (u32[32]{0:T(128)S(1)}, u32[32]{0:T(128)}, u32[]{:S(2)}) copy-start(u32[32]{0:T(128)} %constant.99) | copy-start | bytes 388
  36.8 8.1 %copy-start = (f32[3,32,4096]{2,1,0:T(8,128)}, f32[3,32,4096]{2,1,0:T(8,128)S(1)}, u32[]{:S(2)}) copy-start(f32[3,32,4096]{2,1,0:T(8,128)S(1)} %get-tuple-element.308) | copy-start | bytes 4718596 | tf_op jit(solution)/shard_map/while
  64.4 14.8 %copy-start.1 = (f32[3,32,4096]{2,1,0:T(8,128)S(1)}, f32[3,32,4096]{2,1,0:T(8,128)}, u32[]{:S(2)}) copy-start(f32[3,32,4096]{2,1,0:T(8,128)} %copy-done) | copy-start | bytes 4718596 | tf_op jit(solution)/shard_map/while
  79.2 8.2 %copy-start = (f32[3,32,4096]{2,1,0:T(8,128)}, f32[3,32,4096]{2,1,0:T(8,128)S(1)}, u32[]{:S(2)}) copy-start(f32[3,32,4096]{2,1,0:T(8,128)S(1)} %get-tuple-element.308) | copy-start | bytes 4718596 | tf_op jit(solution)/shard_map/while
  106.8 14.8 %copy-start.1 = (f32[3,32,4096]{2,1,0:T(8,128)S(1)}, f32[3,32,4096]{2,1,0:T(8,128)}, u32[]{:S(2)}) copy-start(f32[3,32,4096]{2,1,0:T(8,128)} %copy-done) | copy-start | bytes 4718596 | tf_op jit(solution)/shard_map/while
  121.6 8.2 %copy-start = (f32[3,32,4096]{2,1,0:T(8,128)}, f32[3,32,4096]{2,1,0:T(8,128)S(1)}, u32[]{:S(2)}) copy-start(f32[3,32,4096]{2,1,0:T(8,128)S(1)} %get-tuple-element.308) | copy-start | bytes 4718596 | tf_op jit(solution)/shard_map/while
  149.2 14.8 %copy-start.1 = (f32[3,32,4096]{2,1,0:T(8,128)S(1)}, f32[3,32,4096]{2,1,0:T(8,128)}, u32[]{:S(2)}) copy-start(f32[3,32,4096]{2,1,0:T(8,128)} %copy-done) | copy-start | bytes 4718596 | tf_op jit(solution)/shard_map/while
  164.0 8.2 %copy-start = (f32[3,32,4096]{2,1,0:T(8,128)}, f32[3,32,4096]{2,1,0:T(8,128)S(1)}, u32[]{:S(2)}) copy-start(f32[3,32,4096]{2,1,0:T(8,128)S(1)} %get-tuple-element.308) | copy-start | bytes 4718596 | tf_op jit(solution)/shard_map/while
  191.5 14.8 %copy-start.1 = (f32[3,32,4096]{2,1,0:T(8,128)S(1)}, f32[3,32,4096]{2,1,0:T(8,128)}, u32[]{:S(2)}) copy-start(f32[3,32,4096]{2,1,0:T(8,128)} %copy-done) | copy-start | bytes 4718596 | tf_op jit(solution)/shard_map/while
  206.4 8.2 %copy-start = (f32[3,32,4096]{2,1,0:T(8,128)}, f32[3,32,4096]{2,1,0:T(8,128)S(1)}, u32[]{:S(2)}) copy-start(f32[3,32,4096]{2,1,0:T(8,128)S(1)} %get-tuple-element.308) | copy-start | bytes 4718596 | tf_op jit(solution)/shard_map/while
  233.9 14.8 %copy-start.1 = (f32[3,32,4096]{2,1,0:T(8,128)S(1)}, f32[3,32,4096]{2,1,0:T(8,128)}, u32[]{:S(2)}) copy-start(f32[3,32,4096]{2,1,0:T(8,128)} %copy-done) | copy-start | bytes 4718596 | tf_op jit(solution)/shard_map/while
  248.7 8.2 %copy-start = (f32[3,32,4096]{2,1,0:T(8,128)}, f32[3,32,4096]{2,1,0:T(8,128)S(1)}, u32[]{:S(2)}) copy-start(f32[3,32,4096]{2,1,0:T(8,128)S(1)} %get-tuple-element.308) | copy-start | bytes 4718596 | tf_op jit(solution)/shard_map/while
  276.3 14.8 %copy-start.1 = (f32[3,32,4096]{2,1,0:T(8,128)S(1)}, f32[3,32,4096]{2,1,0:T(8,128)}, u32[]{:S(2)}) copy-start(f32[3,32,4096]{2,1,0:T(8,128)} %copy-done) | copy-start | bytes 4718596 | tf_op jit(solution)/shard_map/while
  291.2 8.2 %copy-start = (f32[3,32,4096]{2,1,0:T(8,128)}, f32[3,32,4096]{2,1,0:T(8,128)S(1)}, u32[]{:S(2)}) copy-start(f32[3,32,4096]{2,1,0:T(8,128)S(1)} %get-tuple-element.308) | copy-start | bytes 4718596 | tf_op jit(solution)/shard_map/while
  318.8 14.8 %copy-start.1 = (f32[3,32,4096]{2,1,0:T(8,128)S(1)}, f32[3,32,4096]{2,1,0:T(8,128)}, u32[]{:S(2)}) copy-start(f32[3,32,4096]{2,1,0:T(8,128)} %copy-done) | copy-start | bytes 4718596 | tf_op jit(solution)/shard_map/while
  333.6 8.2 %copy-start = (f32[3,32,4096]{2,1,0:T(8,128)}, f32[3,32,4096]{2,1,0:T(8,128)S(1)}, u32[]{:S(2)}) copy-start(f32[3,32,4096]{2,1,0:T(8,128)S(1)} %get-tuple-element.308) | copy-start | bytes 4718596 | tf_op jit(solution)/shard_map/while
  361.2 14.8 %copy-start.1 = (f32[3,32,4096]{2,1,0:T(8,128)S(1)}, f32[3,32,4096]{2,1,0:T(8,128)}, u32[]{:S(2)}) copy-start(f32[3,32,4096]{2,1,0:T(8,128)} %copy-done) | copy-start | bytes 4718596 | tf_op jit(solution)/shard_map/while
  377.1 7.1 %collective-permute-start.3 = (f32[3,1,1024]{2,1,0:T(1,128)S(1)}, f32[3,1,1024]{2,1,0:T(1,128)S(1)}, u32[]{:S(2)}, u32[]{:S(2)}) collective-permute-start(f32[3,1,1024]{2,1,0:T(1,128)S(1)} %get-tuple-element.128), channel_id=1, source_target_pairs={{0,4},{4,8},{8,12},{12,16},{16,20},{20,24},{24,28},{1,5},{5,9},{9,... | collective-permute-start | bytes 36872 | tf_op jit(solution)/shard_map/ppermute | solution.py:34
  379.0 5.9 %collective-permute-start.4 = (f32[3,1,1024]{2,1,0:T(1,128)S(1)}, f32[3,1,1024]{2,1,0:T(1,128)S(1)}, u32[]{:S(2)}, u32[]{:S(2)}) collective-permute-start(f32[3,1,1024]{2,1,0:T(1,128)S(1)} %get-tuple-element.129), channel_id=1, source_target_pairs={{4,0},{8,4},{12,8},{16,12},{20,16},{24,20},{28,24},{5,1},{9,5},{13... | collective-permute-start | bytes 36872 | tf_op jit(solution)/shard_map/ppermute | solution.py:36
  (1 other events, 0.7 us)
